TPU v7x, 32 devices: a whole 2x2x4 slice. The times are simulated.
32 devices in a mesh: dp: 2 (over y), expert: 4 (over z), ffn: 4 (over x, core).
Axes of the slice: x: 2, y: 2, z: 4, core: 2. Of those that a mesh axis runs over, the one named last changes fastest.
Arguments:
- tokens: bfloat16 [64, 6144], P(('dp', 'expert'), 'ffn'), may hold values from -6 to 6
- out_grad: bfloat16 [64, 6144], P(('dp', 'expert'), 'ffn'), may hold values from -6 to 6
- expert_ids: int32 [64, 2], P(('dp', 'expert')), may hold values from 0 to 3, all different within a row; in each aligned block of 8 rows (0 to 7, 8 to 15, ...) at most 6 rows name the same one
- tenant_ids: int32 [64], P(('dp', 'expert')), may hold values from 0 to 7
- router_logits: float32 [64, 2], P(('dp', 'expert')), may hold values from -8 to 8
- gate_projection_weight: bfloat16 [4, 6144, 8192], P('expert', None, ('dp', 'ffn')), may hold values from -0.078125 to 0.078125
- up_projection_weight: bfloat16 [4, 6144, 8192], P('expert', None, ('dp', 'ffn')), may hold values from -0.078125 to 0.078125
- down_projection_weight: bfloat16 [4, 8192, 6144], P('expert', ('dp', 'ffn')), may hold values from -0.0625 to 0.0625
- input_down_maps: bfloat16 [4, 6144, 256], P('expert', 'ffn'), may hold values from -0.078125 to 0.078125
- input_up_maps: bfloat16 [4, 2, 128, 8192], P('expert', None, None, ('dp', 'ffn')), may hold values from -1.5 to 1.5
- output_down_map: bfloat16 [4, 8192, 128], P('expert', ('dp', 'ffn')), may hold values from -0.0625 to 0.0625
- output_up_map: bfloat16 [4, 128, 6144], P('expert', None, 'ffn'), may hold values from -1.5 to 1.5
Outputs:
- mixed: bfloat16 [64, 6144], P(('dp', 'expert'), 'ffn')
- input_grad: bfloat16 [64, 6144], P(('dp', 'expert'), 'ffn')
- input_down_gradient: float32 [4, 6144, 256], P('expert', 'ffn')
- input_up_gradient: float32 [4, 2, 128, 8192], P('expert', None, None, ('dp', 'ffn'))
- output_down_gradient: float32 [4, 8192, 128], P('expert', ('dp', 'ffn'))
- output_up_gradient: float32 [4, 128, 6144], P('expert', None, 'ffn')
Inputs may be any that keep to these rules, and one draw needn't show every extreme that they name: `expert_ids`: each row names 2 different experts. Among the rows of one device's block of 8 tokens no expert is named more than 6 times; in some blocks one expert is named exactly 6 times.
All inputs are finite; a program needn't handle non-finite values.
Results may differ from a plain program's by a relative error of at most 0.0073.
Values may be sent and summed in bfloat16 or wider, within the bound.
A program may use at most 256 MiB of HBM per device.

v0:
```python
import functools

import jax
import jax.numpy as jnp
from jax import lax
from jax.experimental import pallas as pl
from jax.experimental.pallas import tpu as pltpu
from jax.sharding import PartitionSpec as P

RANK = 16
SCALE = 0.5
F32 = jnp.float32
BF16 = jnp.bfloat16
HIGH = lax.Precision.HIGHEST


def dot(a, b, dims=((1,), (0,)), precision=None):
    return lax.dot_general(
        a, b, (dims, ((), ())), preferred_element_type=F32, precision=precision
    )


def dot_nt(a, b, precision=None):
    return dot(a, b, ((1,), (1,)), precision)


def dot_tn(a, b):
    return dot(a, b, ((0,), (0,)))


def flip(index, mask):
    bit = 1
    while bit <= mask:
        if mask & bit:
            index = index + bit - 2 * bit * ((index // bit) % 2)
        bit *= 2
    return index


def bits_of(size):
    assert size & (size - 1) == 0
    return [1 << i for i in range(size.bit_length() - 1)]


def combos(bits):
    out = [0]
    for b in bits:
        out = out + [m | b for m in out]
    return out


def layer_kernel(
    nd, ne, nf,
    src, msk, wg_hbm, wu_hbm, wd_hbm, idm, iup, odm, oum,
    home_o, x_o, y_o, hid, dgr, dur, q_s, vq_s, qz_s, wq_s,
    gath, masks, xb, yb, wg, wu, wd, gate, up, back, home,
    ar1s, ar1r, ar2s, ar2r, *rest,
):
    fbits, dbits = bits_of(nf), bits_of(nd)
    n_rs = len(fbits) + len(dbits)
    yr, xr = rest[:n_rs], rest[n_rs : 2 * n_rs]
    wsem, lsem, ssem, rsem = rest[2 * n_rs :]
    d, e, f = lax.axis_index("dp"), lax.axis_index("expert"), lax.axis_index("ffn")
    quarter = src.shape[2]
    hidden = wg.shape[2]
    rows_d = ne * 8
    rows = nd * rows_d
    cw = min(256, hidden)
    n_hc = hidden // cw
    qw = 256 if quarter % 256 == 0 else 128
    n_qc = quarter // qw
    pending = []
    counter = [0]

    def send(s, t, dev):
        i = counter[0]
        counter[0] += 1
        c = pltpu.make_async_remote_copy(
            src_ref=s, dst_ref=t, send_sem=ssem.at[i], recv_sem=rsem.at[i],
            device_id=dev, device_id_type=pl.DeviceIdType.MESH,
        )
        c.start()
        pending.append(c)
        return c

    arrival = [0]
    for b in reversed(fbits):
        arrival = arrival + [m | b for m in arrival]
    wcopies = []
    k = 0
    for m in arrival:
        qq = flip(f, m)
        pair = []
        for hbm, v in ((wg_hbm, wg), (wu_hbm, wu)):
            c = pltpu.make_async_copy(
                hbm.at[0, pl.ds(pl.multiple_of(qq * quarter, 128), quarter), :],
                v.at[qq], wsem.at[k],
            )
            c.start()
            k += 1
            pair.append(c)
        wcopies.append(pair)
    wd_copy = pltpu.make_async_copy(wd_hbm.at[0], wd, wsem.at[k])
    wd_copy.start()

    own = [
        pltpu.make_async_copy(src.at[e], gath.at[f, d, e], lsem.at[0]),
        pltpu.make_async_copy(msk.at[e], masks.at[d, e], lsem.at[1]),
    ]
    for c in own:
        c.start()

    barrier = pltpu.get_barrier_semaphore()
    peers = [(d, (e + j) % ne, f) for j in range(1, ne)]
    peers += [(flip(d, b), e, f) for b in dbits]
    peers += [(d, e, flip(f, b)) for b in fbits]
    for p in peers:
        pl.semaphore_signal(barrier, inc=1, device_id=p, device_id_type=pl.DeviceIdType.MESH)
    pl.semaphore_wait(barrier, len(peers))

    got = []
    for j in range(1, ne):
        to = (e + j) % ne
        got.append(send(src.at[to], gath.at[f, d, e], (d, to, f)))
        got.append(send(msk.at[to], masks.at[d, e], (d, to, f)))
    for c in own:
        c.wait()
    for c in got:
        c.wait_recv()

    top = fbits[-1] if fbits else 0
    early = []
    if top:
        early.append(send(gath.at[f, d], gath.at[f, d], (d, e, flip(f, top))))
    held = [0]
    for b in dbits:
        got = []
        for m in held:
            dm = flip(d, m)
            got.append(send(gath.at[f, dm], gath.at[f, dm], (flip(d, b), e, f)))
            got.append(send(masks.at[dm], masks.at[dm], (flip(d, b), e, f)))
        for c in got:
            c.wait_recv()
        if top:
            for m in held:
                dm = flip(d, b | m)
                early.append(send(gath.at[f, dm], gath.at[f, dm], (d, e, flip(f, top))))
        held = held + [m | b for m in held]

    half = ne // 2
    ys, xs = gath.at[:, :, :half], gath.at[:, :, half:]

    def unpack(q):
        def body(p, carry):
            dd, ee = p // half, (p % half) * 2
            v0 = gath[q, dd, ee].astype(F32)
            v1 = gath[q, dd, ee + 1].astype(F32)
            at = pl.ds(pl.multiple_of(p * 16, 16), 16)
            xb[q, at, :] = jnp.concatenate([v0[:8], v1[:8]], axis=0).astype(BF16)
            yb[q, at, :] = jnp.concatenate([v0[8:], v1[8:]], axis=0).astype(BF16)
            return carry

        lax.fori_loop(0, nd * half, body, 0)

    mask = masks[...].reshape(rows, masks.shape[3])
    ntr = mask.shape[1]
    mask3 = jnp.concatenate([mask, mask, mask], axis=1)
    lanes = 128
    col = lax.broadcasted_iota(jnp.int32, (3 * ntr, lanes), 0)
    lane = lax.broadcasted_iota(jnp.int32, (3 * ntr, lanes), 1)
    select = ((col // ntr) * RANK + col % RANK == lane).astype(F32)

    def compress(v):
        return dot(v * mask3, select, precision=HIGH)

    def expand(v):
        return dot_nt(v, select, precision=HIGH) * mask3

    def all_reduce(v, axes, sbuf, rbuf):
        for i, (axis, b) in enumerate(axes):
            sbuf[i] = v
            dev = (d, e, flip(f, b)) if axis == "f" else (flip(d, b), e, f)
            c = send(sbuf.at[i], rbuf.at[i], dev)
            yield
            c.wait_recv()
            v = v + rbuf[i]
        yield v

    def finish(gen):
        v = None
        for v in gen:
            pass
        return v

    unpack(f)
    pv = jnp.concatenate([dot(xb[f], idm[0]), dot_nt(yb[f], oum[0])], axis=1)
    ar1 = all_reduce(compress(pv), [("f", b) for b in reversed(fbits)], ar1s, ar1r)
    next(ar1)

    def project(m, first):
        q = flip(f, m)
        wcopies[arrival.index(m)][0].wait()
        wcopies[arrival.index(m)][1].wait()

        def body(c, carry):
            at = pl.ds(pl.multiple_of(c * cw, cw), cw)
            x = xb[q]
            g = dot(x, wg[q, :, at])
            u = dot(x, wu[q, :, at])
            if first:
                gate[:, at] = g
                up[:, at] = u
            else:
                gate[:, at] += g
                up[:, at] += u
            return carry

        lax.fori_loop(0, n_hc, body, 0)

    project(0, True)
    ready = [0]
    for n, b in enumerate(reversed(fbits)):
        if n == 0:
            got = early
        else:
            got = []
            for m in ready:
                qm = flip(f, m)
                got.append(send(gath.at[qm], gath.at[qm], (d, e, flip(f, b))))
        for c in got:
            c.wait_recv()
        ready = ready + [m | b for m in ready]
        if n + 1 < len(fbits):
            continue
    v = finish(ar1)
    pv = expand(v)
    q_s[...] = pv[:, : 2 * ntr].astype(BF16)
    vq_s[...] = pv[:, 2 * ntr :].astype(BF16)
    for m in arrival[1:]:
        unpack(flip(f, m))
        project(m, False)

    def activate(c, carry):
        at = pl.ds(pl.multiple_of(c * cw, cw), cw)
        g = gate[:, at] + SCALE * dot(q_s[:, :ntr], iup[0, 0, :, at])
        u = up[:, at] + SCALE * dot(q_s[:, ntr:], iup[0, 1, :, at])
        gate[:, at] = g
        up[:, at] = u
        hid[:, at] = (g * jax.nn.sigmoid(g) * u).astype(BF16)
        return carry

    lax.fori_loop(0, n_hc, activate, 0)

    def reduce_scatter(slabs, rbufs, produce):
        rec = {}
        for i, b in enumerate(fbits):
            ms = combos(fbits[i + 1 :])
            for n, m in enumerate(ms):
                add(slabs, rec, rbufs, i, b | m, produce)
                q = flip(f, b | m)
                rec[(i, m)] = (send(slabs.at[q], rbufs[i].at[n], (d, e, flip(f, b))), n)
                yield
        add(slabs, rec, rbufs, len(fbits), 0, produce)
        yield
        drec = {}
        for i, b in enumerate(dbits):
            r = rbufs[len(fbits) + i]
            ms = combos(dbits[i + 1 :])
            for n, m in enumerate(ms):
                dm = flip(d, b | m)
                for j in range(i):
                    c, pos = drec[(j, b | m)]
                    c.wait_recv()
                    slabs[f, dm] = (
                        slabs[f, dm].astype(F32) + rbufs[len(fbits) + j][pos].astype(F32)
                    ).astype(BF16)
                drec[(i, m)] = (send(slabs.at[f, dm], r.at[n], (flip(d, b), e, f)), n)
        yield
        total = slabs[f, d].astype(F32)
        for i in range(len(dbits)):
            c, pos = drec[(i, 0)]
            c.wait_recv()
            total = total + rbufs[len(fbits) + i][pos].astype(F32)
        yield total.reshape(rows_d, quarter)

    def add(slabs, rec, rbufs, upto, m, produce):
        q = flip(f, m)
        produce(q)
        for j in range(upto):
            c, pos = rec[(j, m)]
            c.wait_recv()
            slabs[q] = (slabs[q].astype(F32) + rbufs[j][pos].astype(F32)).astype(BF16)

    wd_copy.wait()
    for c in pending:
        c.wait_send()
    pending.clear()

    def produce_y(q):
        def body(c, carry):
            at = pl.ds(pl.multiple_of(c * qw, qw), qw)
            v = dot(hid[...], wd[:, pl.ds(pl.multiple_of(q * quarter + c * qw, qw), qw)])
            ys[q, :, :, :, at] = v.astype(BF16).reshape(nd, half, 16, qw)
            return carry

        lax.fori_loop(0, n_qc, body, 0)

    def produce_x(q):
        def body(c, carry):
            at = pl.ds(pl.multiple_of(c * qw, qw), qw)
            v = dot_nt(dgr[...], wg[q, at, :]) + dot_nt(dur[...], wu[q, at, :])
            xs[q, :, :, :, at] = v.astype(BF16).reshape(nd, half, 16, qw)
            return carry

        lax.fori_loop(0, n_qc, body, 0)

    y_gen = reduce_scatter(ys, yr, produce_y)
    for _ in range(nf):
        next(y_gen)
    z = dot(hid[...], odm[0])

    def backward(c, carry):
        at = pl.ds(pl.multiple_of(c * cw, cw), cw)
        dh = SCALE * dot_nt(vq_s[...], odm[0, at, :])
        for q in range(nf):
            dh = dh + dot_nt(yb[q], wd[at, q * quarter : (q + 1) * quarter])
        g = gate[:, at]
        s = jax.nn.sigmoid(g)
        dgr[:, at] = (dh * up[:, at] * s * (1.0 + g * (1.0 - s))).astype(BF16)
        dur[:, at] = (dh * (g * s)).astype(BF16)
        return carry

    lax.fori_loop(0, n_hc, backward, 0)
    next(y_gen)
    w0 = dot_nt(dgr[...], iup[0, 0])
    w1 = dot_nt(dur[...], iup[0, 1])
    ar2 = all_reduce(
        compress(jnp.concatenate([z, w0, w1], axis=1)),
        [("f", b) for b in fbits] + [("d", b) for b in dbits], ar2s, ar2r,
    )
    next(ar2)
    x_gen = reduce_scatter(xs, xr, produce_x)
    zw = None
    for _ in range(nf):
        next(x_gen)
        if zw is None:
            zw = next(ar2)
    while zw is None:
        zw = next(ar2)
    next(x_gen)
    zw = expand(zw)
    qz_s[...] = zw[:, :ntr].astype(BF16)
    wq_s[...] = zw[:, ntr:].astype(BF16)

    mine = pl.ds(pl.multiple_of(d * rows_d, 16), rows_d)
    y_add = SCALE * dot(qz_s[mine, :], oum[0])
    x_add = SCALE * dot_nt(wq_s[mine, :], idm[0])
    y_own = next(y_gen) + y_add
    x_own = next(x_gen) + x_add
    for j in range(ne):
        at = slice(j * 8, j * 8 + 8)
        back[j] = jnp.concatenate([y_own[at], x_own[at]], axis=0).astype(BF16)
    home_own = pltpu.make_async_copy(back.at[e], home.at[e], lsem.at[2])
    home_own.start()
    got = []
    for j in range(1, ne):
        to = (e + j) % ne
        got.append(send(back.at[to], home.at[e], (d, to, f)))

    x_o[...] = xb[f]
    y_o[...] = yb[f]
    home_own.wait()
    for c in got:
        c.wait_recv()
    home_o[...] = home[...]
    for c in pending:
        c.wait_send()


def output_kernel(
    wts, home, xp, yp, hid, dgr, dur, q_s, vq_s, qz_s, wq_s,
    mixed, igrad, idg, iug, odg, oug,
):
    ntr = vq_s.shape[1]
    idg[0] = SCALE * dot_tn(xp[...], wq_s[...])
    oug[0] = SCALE * dot_tn(qz_s[...], yp[...])
    odg[0] = SCALE * dot_tn(hid[...], vq_s[...])
    iug[0, 0] = SCALE * dot_tn(q_s[:, :ntr], dgr[...])
    iug[0, 1] = SCALE * dot_tn(q_s[:, ntr:], dur[...])
    out = jnp.zeros(mixed.shape, F32)
    grad = jnp.zeros(mixed.shape, F32)
    for j in range(home.shape[0]):
        v = home[j].astype(F32)
        out = out + wts[j, :, :1] * v[:8]
        grad = grad + v[8:]
    mixed[...] = out.astype(BF16)
    igrad[...] = grad.astype(BF16)


def per_device(
    tokens, out_grad, expert_ids, tenant_ids, router_logits,
    gate_projection_weight, up_projection_weight, down_projection_weight,
    input_down_maps, input_up_maps, output_down_map, output_up_map,
):
    ne, nd, nf = lax.axis_size("expert"), lax.axis_size("dp"), lax.axis_size("ffn")
    tok, quarter = tokens.shape
    hidden = gate_projection_weight.shape[2]
    ntr = output_down_map.shape[2]
    rows_d = ne * tok
    rows = nd * rows_d
    first = jax.nn.sigmoid(router_logits[:, 0] - router_logits[:, 1])
    probs = jnp.stack([first, 1.0 - first], axis=1)
    hit = expert_ids[None] == jnp.arange(ne, dtype=jnp.int32)[:, None, None]
    member = jnp.any(hit, axis=2)
    weight = jnp.sum(jnp.where(hit, probs[None], 0.0), axis=2)
    x = jnp.where(member[:, :, None], tokens[None], jnp.zeros((), BF16))
    dy = (weight[:, :, None] * out_grad.astype(F32)[None]).astype(BF16)
    src = jnp.concatenate([x, dy], axis=1)
    column = jnp.arange(ntr, dtype=jnp.int32) // RANK
    msk = (member[:, :, None] & (tenant_ids[None, :, None] == column[None, None])).astype(F32)
    wts = jnp.broadcast_to(weight[:, :, None], (ne, tok, 128))

    fbits, dbits = bits_of(nf), bits_of(nd)
    rs_bufs = [pltpu.VMEM((nf >> (i + 1), nd, ne // 2, 16, quarter), BF16) for i in range(len(fbits))]
    rs_bufs += [pltpu.VMEM((nd >> (i + 1), ne // 2, 16, quarter), BF16) for i in range(len(dbits))]
    n_sem = (
        3 * (ne - 1) + 3 * nd + nf + 2 * (nf + nd) + 2 * len(fbits) + len(dbits)
    )
    n1, n2 = max(len(fbits), 1), max(len(fbits) + len(dbits), 1)
    vmem = pl.BlockSpec(memory_space=pltpu.VMEM)
    hbm = pl.BlockSpec(memory_space=pl.ANY)
    parts = pl.pallas_call(
        functools.partial(layer_kernel, nd, ne, nf),
        out_shape=(
            jax.ShapeDtypeStruct(src.shape, BF16),
            jax.ShapeDtypeStruct((rows, quarter), BF16),
            jax.ShapeDtypeStruct((rows, quarter), BF16),
            jax.ShapeDtypeStruct((rows, hidden), BF16),
            jax.ShapeDtypeStruct((rows, hidden), BF16),
            jax.ShapeDtypeStruct((rows, hidden), BF16),
            jax.ShapeDtypeStruct((rows, 2 * ntr), BF16),
            jax.ShapeDtypeStruct((rows, ntr), BF16),
            jax.ShapeDtypeStruct((rows, ntr), BF16),
            jax.ShapeDtypeStruct((rows, 2 * ntr), BF16),
        ),
        in_specs=[vmem] * 2 + [hbm] * 3 + [vmem] * 4,
        out_specs=[vmem] * 10,
        scratch_shapes=[
            pltpu.VMEM((nf, nd, ne, 2 * tok, quarter), BF16),
            pltpu.VMEM((nd, ne, tok, ntr), F32),
            pltpu.VMEM((nf, rows, quarter), BF16),
            pltpu.VMEM((nf, rows, quarter), BF16),
            pltpu.VMEM((nf, quarter, hidden), BF16),
            pltpu.VMEM((nf, quarter, hidden), BF16),
            pltpu.VMEM((hidden, nf * quarter), BF16),
            pltpu.VMEM((rows, hidden), F32),
            pltpu.VMEM((rows, hidden), F32),
            pltpu.VMEM((ne, 2 * tok, quarter), BF16),
            pltpu.VMEM((ne, 2 * tok, quarter), BF16),
            pltpu.VMEM((n1, rows, 128), F32),
            pltpu.VMEM((n1, rows, 128), F32),
            pltpu.VMEM((n2, rows, 128), F32),
            pltpu.VMEM((n2, rows, 128), F32),
            *rs_bufs,
            *rs_bufs,
            pltpu.SemaphoreType.DMA((2 * nf + 1,)),
            pltpu.SemaphoreType.DMA((3,)),
            pltpu.SemaphoreType.DMA((n_sem,)),
            pltpu.SemaphoreType.DMA((n_sem,)),
        ],
        compiler_params=pltpu.CompilerParams(
            collective_id=0, has_side_effects=True, vmem_limit_bytes=67043328
        ),
    )(
        src, msk,
        gate_projection_weight, up_projection_weight, down_projection_weight,
        input_down_maps, input_up_maps, output_down_map, output_up_map,
    )
    return pl.pallas_call(
        output_kernel,
        out_shape=(
            jax.ShapeDtypeStruct(tokens.shape, BF16),
            jax.ShapeDtypeStruct(tokens.shape, BF16),
            jax.ShapeDtypeStruct(input_down_maps.shape, F32),
            jax.ShapeDtypeStruct(input_up_maps.shape, F32),
            jax.ShapeDtypeStruct(output_down_map.shape, F32),
            jax.ShapeDtypeStruct(output_up_map.shape, F32),
        ),
        in_specs=[vmem] * 11,
        out_specs=[vmem] * 6,
    )(wts, *parts)


def solution(mesh):
    return jax.shard_map(
        per_device,
        mesh=mesh,
        in_specs=(
            P(("dp", "expert"), "ffn"),
            P(("dp", "expert"), "ffn"),
            P(("dp", "expert"), None),
            P(("dp", "expert")),
            P(("dp", "expert"), None),
            P("expert", None, ("dp", "ffn")),
            P("expert", None, ("dp", "ffn")),
            P("expert", ("dp", "ffn"), None),
            P("expert", "ffn", None),
            P("expert", None, None, ("dp", "ffn")),
            P("expert", ("dp", "ffn"), None),
            P("expert", None, "ffn"),
        ),
        out_specs=(
            P(("dp", "expert"), "ffn"),
            P(("dp", "expert"), "ffn"),
            P("expert", "ffn", None),
            P("expert", None, None, ("dp", "ffn")),
            P("expert", ("dp", "ffn"), None),
            P("expert", None, "ffn"),
        ),
        check_vma=False,
    )
```

profile of v0, /device:TPU:0, one launch (start us, length us, event | category | flops | bytes accessed | tf_op | source)
XLA Modules:
  0.0 81.7 jit_solution(6117940816796048074)
XLA Ops:
  0.6 0.7 fusion
  1.3 0.7 broadcast_compare_fusion
  2.1 0.8 broadcast_subtract_fusion
  2.8 0.7 select_reduce_fusion
  3.5 0.7 and_convert_fusion.msk
  4.2 0.7 broadcast_in_dim.50.wts
  4.9 0.7 convert_element_type.9
  5.6 0.1 multiply_convert_fusion
  5.7 0.8 %broadcast_select_fusion = bf16[4,8,1536]{2,1,0:T(8,128)(2,1)S(1)} fusion(pred[4,8]{1,0:T(4,128)(4,1)S(1)} %fusion, bf16[8,1536]{1,0:T(8,128)(2,1)} %param.12), kind=kLoop, calls=%fused_computation.2 | loop fusion | flops 49152 | bytes 122912 | tf_op jit(solution)/shard_map/jit(_where)/select_n | solution.py:416
  6.5 0.7 pad_maximum_fusion.src
  7.2 70.8 %shard_map.163 = (bf16[4,16,1536]{2,1,0:T(8,128)(2,1)}, bf16[64,1536]{1,0:T(8,128)(2,1)}, bf16[64,1536]{1,0:T(8,128)(2,1)}, bf16[64,1024]{1,0:T(8,128)(2,1)}, bf...) custom-call(bf16[4,16,1536]{2,1,0:T(8,128)(2,1)} %pad_maximum_fusion, ...), custom_call_target="tpu_custom_call" | custom-call | tf_op jit(solution)/shard_map/pallas_call | solution.py:432
  78.0 3.7 %shard_map.164 = (bf16[8,1536]{1,0:T(8,128)(2,1)}, bf16[8,1536]{1,0:T(8,128)(2,1)}, f32[1,1536,256]{2,1,0:T(8,128)}, f32[1,2,128,1024]{3,2,1,0:T(8,128)}, f32[1,...) custom-call(f32[4,8,128]{2,1,0:T(8,128)} %broadcast_in_dim.50.wts, bf16[4,16,1536]{2,1,0:T(8,128)(2,1)} %get-tuple-element.16.home, ...), custom_call_target="tpu_custom_call" | custom-call | tf_op jit(solution)/shard_map/pallas_call | solution.py:479
  (2 shorter events, 0.0 us)
where the time goes:
time: 82 us; the launch traced here: 81.7 us
  Pallas kernels  74.5 us (91%)
  other arithmetic  5.9 us (7%)
    pallas_call x1, Pallas kernels, per_device(): pl.pallas_call(functools.partial(layer_kernel, nd, ne, nf), out_shape=(ja...  70.8 us
    pallas_call x1, Pallas kernels, per_device(): pl.pallas_call(output_kernel, out_shape=(jax.ShapeDtypeStruct(tokens.shap...  3.69 us

commit v1 on v0

v1 whole, which is shorter than its diff:
```python
import functools

import jax
import jax.numpy as jnp
from jax import lax
from jax.experimental import pallas as pl
from jax.experimental.pallas import tpu as pltpu
from jax.sharding import PartitionSpec as P

RANK = 16
SCALE = 0.5
F32 = jnp.float32
BF16 = jnp.bfloat16
HIGH = lax.Precision.HIGHEST
LANES = 128


def dot(a, b, dims=((1,), (0,)), precision=None):
    return lax.dot_general(
        a, b, (dims, ((), ())), preferred_element_type=F32, precision=precision
    )


def dot_nt(a, b, precision=None):
    return dot(a, b, ((1,), (1,)), precision)


def dot_tn(a, b):
    return dot(a, b, ((0,), (0,)))


def flip(index, mask):
    bit = 1
    while bit <= mask:
        if mask & bit:
            index = index + bit - 2 * bit * ((index // bit) % 2)
        bit *= 2
    return index


def bits_of(size):
    assert size & (size - 1) == 0
    return [1 << i for i in range(size.bit_length() - 1)]


def orders(nd, nf):
    fb = [("f", b) for b in reversed(bits_of(nf))]
    db = [("d", b) for b in reversed(bits_of(nd))]
    core = fb[-1:]
    return (fb[:-1] + db + core, db + fb[:-1] + core)


def stages(dims, mask):
    return [i for i, (a, b) in enumerate(dims) if mask[0 if a == "f" else 1] & b]


def step(mask, dim):
    a, b = dim
    return (mask[0] ^ b, mask[1]) if a == "f" else (mask[0], mask[1] ^ b)


def all_masks(nd, nf):
    return [(mf, r) for mf in range(nf) for r in range(nd)]


def received(dims, i, nd, nf):
    return [m for m in all_masks(nd, nf) if all(j > i for j in stages(dims, m))]


def layer_kernel(
    nd, ne, nf, tok,
    tokens, out_grad, ids, tids, logits, wg_hbm, wu_hbm, wd_hbm, idm_hbm, iup_hbm, odm_hbm, oum_hbm,
    mixed, igrad, idg, iug, odg, oug,
    tok_v, grad_v, ids_v, tids_v, logits_v, idm, iup, odm, oum,
    src, msrc, wts, held, masks, wg, wu, wd, gate, up, dh, hid, dgr, dur,
    part, rcore, back, home, ar1s, ar1r, ar2s, ar2r, *rest,
):
    routes = orders(nd, nf)
    core = routes[0][-1]
    rsd = [[core] + [x for x in r if x != core] for r in routes]
    rbuf = {}
    n = 0
    for h in range(2):
        for i in range(1, len(rsd[h])):
            rbuf[h, i] = rest[n]
            n += 1
    isem, wsem, ssem, rsem = rest[n:]
    d, e, f = lax.axis_index("dp"), lax.axis_index("expert"), lax.axis_index("ffn")
    quarter = tokens.shape[1]
    hidden = gate.shape[1]
    rows_d = ne * tok
    rows = nd * rows_d
    half = quarter // 2
    ntr = odm.shape[1]
    pending = []
    counter = [0]

    def peer(dim):
        a, b = dim
        return (d, e, flip(f, b)) if a == "f" else (flip(d, b), e, f)

    def send(s, t, dev):
        i = counter[0]
        counter[0] += 1
        c = pltpu.make_async_remote_copy(
            src_ref=s, dst_ref=t, send_sem=ssem.at[i], recv_sem=rsem.at[i],
            device_id=dev, device_id_type=pl.DeviceIdType.MESH,
        )
        c.start()
        pending.append(c)
        return c

    barrier = pltpu.get_barrier_semaphore()
    peers = [(d, flip(e, m), f) for m in range(1, ne)] + [peer(x) for x in routes[0]]
    for p in peers:
        pl.semaphore_signal(barrier, inc=1, device_id=p, device_id_type=pl.DeviceIdType.MESH)

    def load(s, t, sem):
        c = pltpu.make_async_copy(s, t, sem)
        c.start()
        return c

    first = [
        load(a, b, isem.at[i])
        for i, (a, b) in enumerate(
            [(ids, ids_v), (tids, tids_v), (logits, logits_v), (tokens, tok_v), (out_grad, grad_v)]
        )
    ]
    for c in first:
        c.wait()
    maps = [
        load(a, b, isem.at[5 + i])
        for i, (a, b) in enumerate(
            [(idm_hbm.at[0], idm), (oum_hbm.at[0], oum), (iup_hbm.at[0], iup), (odm_hbm.at[0], odm)]
        )
    ]
    wcopies = {}
    for m in range(nf):
        at = pl.ds(pl.multiple_of(flip(f, m) * quarter, LANES), quarter)
        wcopies[m] = [
            load(wg_hbm.at[0, at, :], wg.at[m], wsem.at[3 * m]),
            load(wu_hbm.at[0, at, :], wu.at[m], wsem.at[3 * m + 1]),
            load(wd_hbm.at[0, :, at], wd.at[m], wsem.at[3 * m + 2]),
        ]

    eye = lax.broadcasted_iota(jnp.int32, (tok, tok), 0) == lax.broadcasted_iota(jnp.int32, (tok, tok), 1)

    def upright(row):
        return jnp.sum(jnp.where(eye, jnp.broadcast_to(row, (tok, tok)), 0.0), axis=1, keepdims=True)

    lg = logits_v[...]
    p0 = jax.nn.sigmoid(upright(lg[0:1]) - upright(lg[1:2]))
    idv = ids_v[...].astype(F32)
    choice = (upright(idv[0:1]), upright(idv[1:2]))
    tcol = upright(tids_v[...].astype(F32))
    column = (lax.broadcasted_iota(jnp.int32, (tok, ntr), 1) // RANK).astype(F32)
    tmask = (tcol == column).astype(F32)
    tv = tok_v[...].astype(F32)
    gv = grad_v[...].astype(F32)
    for k in range(ne):
        hit = [(c == float(k)).astype(F32) for c in choice]
        member = hit[0] + hit[1]
        weight = hit[0] * p0 + hit[1] * (1.0 - p0)
        src[k, 0] = (tv * member).astype(BF16)
        src[k, 1] = (gv * weight).astype(BF16)
        msrc[k] = tmask * member
        wts[k] = jnp.broadcast_to(weight, (tok, LANES))
    pl.semaphore_wait(barrier, len(peers))

    def block(mf, r, lo, n):
        return held.at[mf, :, pl.ds(r * rows_d + lo * tok, n * tok), :]

    zc = {}
    zm = {}
    for m in range(1, ne):
        to = (d, flip(e, m), f)
        zc[m] = send(src.at[flip(e, m)], block(0, 0, m, 1), to)
    for m in range(1, ne):
        to = (d, flip(e, m), f)
        zm[m] = send(msrc.at[flip(e, m)], masks.at[0, pl.ds(m * tok, tok), :], to)

    arrivals = {}
    hn = max(ne // 2, 1)

    def forward(s, mask, route, lo, n):
        dims = routes[route]
        last = max(stages(dims, mask), default=-1)
        for i in range(last + 1, len(dims)):
            to = step(mask, dims[i])
            c = send(s, block(to[0], to[1], lo, n), peer(dims[i]))
            arrivals.setdefault((to, route), []).append((lo, n, c))

    held[0, :, pl.ds(0, tok), :] = src[e]
    masks[0, pl.ds(0, tok), :] = msrc[e]
    forward(src.at[e], (0, 0), 0, 0, 1)
    znear = [1] + [m for m in range(ne - 1, 1, -1)] if ne > 1 else []
    for m in znear:
        zc[m].wait_recv()
        forward(block(0, 0, m, 1), (0, 0), m // hn, m, 1)

    def pass_on(mask, route):
        for lo, n, c in arrivals[mask, route]:
            c.wait_recv()
            if n == 1 and ne > 4:
                continue
            forward(block(mask[0], mask[1], lo, n), mask, route, lo, n)
        if ne > 4 and arrivals[mask, route][0][1] == 1:
            forward(block(mask[0], mask[1], route * hn, hn), mask, route, route * hn, hn)

    def by_last(mask):
        return [max(stages(routes[h], mask)) for h in range(2)]

    for m in range(1, ne):
        zm[m].wait_recv()
    mc = []
    have = [0]
    for a, b in [x for x in routes[0] if x[0] == "d"]:
        got = [send(masks.at[r], masks.at[r ^ b], peer((a, b))) for r in have]
        mc.append(got)
        have = have + [r ^ b for r in have]
        if len(mc) < len(bits_of(nd)):
            for c in got:
                c.wait_recv()

    todo = [(m, h) for m in all_masks(nd, nf) if m != (0, 0) for h in range(2)]
    todo = [(m, h) for m, h in todo if stages(routes[h], m)[-1] != len(routes[h]) - 1]
    todo.sort(key=lambda t: (len(stages(routes[t[1]], t[0])), stages(routes[t[1]], t[0])[-1]))
    done = set()

    def run_until(need):
        while todo and not all(t in done for t in need):
            m, h = todo.pop(0)
            pass_on(m, h)
            done.add((m, h))

    run_until([((0, r), h) for r in range(1, nd) for h in range(2)])
    for got in mc[-1:]:
        for c in got:
            c.wait_recv()
    for c in maps:
        c.wait()

    mask = masks[...].reshape(rows, ntr)
    mask3 = jnp.concatenate([mask, mask, mask], axis=1)
    col = lax.broadcasted_iota(jnp.int32, (3 * ntr, LANES), 0)
    lane = lax.broadcasted_iota(jnp.int32, (3 * ntr, LANES), 1)
    select = ((col // ntr) * RANK + col % RANK == lane).astype(F32)

    def compress(v):
        return dot(v * mask3, select, precision=HIGH)

    def expand(v):
        return dot_nt(v, select, precision=HIGH) * mask3

    def all_reduce(v, dims, sbuf, rbuf):
        for i, dim in enumerate(dims):
            sbuf[i] = v
            c = send(sbuf.at[i], rbuf.at[i], peer(dim))
            yield None
            c.wait_recv()
            got = rbuf[i]
            if dim[0] == "d":
                got = jnp.concatenate(
                    [got[(r ^ dim[1]) * rows_d : ((r ^ dim[1]) + 1) * rows_d] for r in range(nd)], axis=0
                )
            v = v + got
        yield v

    pv = jnp.concatenate([dot(held[0, 0], idm[...]), dot_nt(held[0, 1], oum[...])], axis=1)
    ar1 = all_reduce(compress(pv), [x for x in routes[0] if x[0] == "f"], ar1s, ar1r)
    next(ar1)

    def project(m, start):
        for c in wcopies[m]:
            c.wait()
        x, y = held[m, 0], held[m, 1]
        g, u, h = dot(x, wg[m]), dot(x, wu[m]), dot_nt(y, wd[m])
        if start:
            gate[...] = g
            up[...] = u
            dh[...] = h
        else:
            gate[...] += g
            up[...] += u
            dh[...] += h

    project(0, True)
    run_until([t for t in todo])
    pv = next(ar1)
    for m in range(1, nf):
        for r in range(nd):
            for h in range(2):
                if max(stages(routes[h], (m, r))) == len(routes[h]) - 1:
                    for _, _, c in arrivals[(m, r), h]:
                        c.wait_recv()
        project(m, False)
        if pv is None:
            pv = next(ar1)
    while pv is None:
        pv = next(ar1)
    pv = expand(pv)
    q = pv[:, : 2 * ntr].astype(BF16)
    vq = pv[:, 2 * ntr :].astype(BF16)

    aw = min(hidden, 256 if rows <= 64 else 128)
    for k in range(hidden // aw):
        at = slice(k * aw, (k + 1) * aw)
        g = gate[:, at] + SCALE * dot(q[:, :ntr], iup[0, :, at])
        u = up[:, at] + SCALE * dot(q[:, ntr:], iup[1, :, at])
        t = dh[:, at] + SCALE * dot_nt(vq, odm[at, :])
        s = jax.nn.sigmoid(g)
        gs = g * s
        hid[:, at] = (gs * u).astype(BF16)
        dgr[:, at] = (t * u * s * (1.0 + g * (1.0 - s))).astype(BF16)
        dur[:, at] = (t * gs).astype(BF16)

    z = dot(hid[...], odm[...])
    w0 = dot_nt(dgr[...], iup[0])
    w1 = dot_nt(dur[...], iup[1])
    ar2 = all_reduce(
        compress(jnp.concatenate([z, w0, w1], axis=1)), list(reversed(routes[0])), ar2s, ar2r
    )
    next(ar2)

    rec = {}

    def cols(h):
        return pl.ds(h * half, half)

    def rowsof(r):
        return pl.ds(r * rows_d, rows_d)

    def produce(k, m):
        if k == 0:
            v = dot(hid[...], wd[m])
        else:
            v = dot_nt(dgr[...], wg[m]) + dot_nt(dur[...], wu[m])
        part[k, m] = v.astype(BF16)
        if m & core[1]:
            rec[k, m ^ core[1]] = send(
                part.at[k, m], rcore.at[k, received_core.index(m ^ core[1])], peer(core)
            )

    received_core = [m for m in range(nf) if not m & core[1]]

    def add_core(k, m):
        rec[k, m].wait_recv()
        part[k, m] = (part[k, m].astype(F32) + rcore[k, received_core.index(m)].astype(F32)).astype(BF16)

    def pieces(k, h, i, only):
        dims = rsd[h]
        for m in all_masks(nd, nf):
            st = stages(dims, m)
            if st and st[0] == i and only(m):
                for j in range(1, i):
                    take(k, h, j, m)
                to = step(m, dims[i])
                slot = received(dims, i, nd, nf).index(to)
                rec[k, h, i, to] = send(
                    part.at[k, m[0], rowsof(m[1]), cols(h)], rbuf[h, i].at[k, slot], peer(dims[i])
                )

    def take(k, h, j, m):
        rec[k, h, j, m].wait_recv()
        slot = received(rsd[h], j, nd, nf).index(m)
        at = (k, m[0], rowsof(m[1]), cols(h))
        part[at] = (part[at].astype(F32) + rbuf[h, j][k, slot].astype(F32)).astype(BF16)

    zret = {}

    def finish(k, h, extra):
        dims = rsd[h]
        total = part[k, 0, rowsof(0), cols(h)].astype(F32)
        for j in range(1, len(dims)):
            rec[k, h, j, (0, 0)].wait_recv()
            slot = received(dims, j, nd, nf).index((0, 0))
            total = total + rbuf[h, j][k, slot].astype(F32)
        total = total + extra[:, h * half : (h + 1) * half]
        back[k, :, cols(h)] = total.astype(BF16)
        for m in range(1, ne):
            zret[k, h, m] = send(
                back.at[k, pl.ds(m * tok, tok), cols(h)], home.at[k, m, :, cols(h)], (d, flip(e, m), f)
            )

    order = sorted(range(nf), key=lambda m: (-(m & ~core[1]), not m & core[1]))
    for m in order:
        produce(0, m)

    def stage_of(k, i):
        for h in range(2):
            pieces(k, h, i, lambda m: True)

    nst = len(rsd[0])
    produce(1, order[0])
    for m in received_core:
        add_core(0, m)
    stage_of(0, 1)
    zw = next(ar2)
    mid = order[1:-1]
    later = list(range(2, nst))
    early1 = [m for m in received_core if m != order[-1]]
    for n, m in enumerate(mid):
        produce(1, m)
        if zw is None:
            zw = next(ar2)
        if m in early1:
            add_core(1, m)
            for h in range(2):
                pieces(1, h, 1, lambda t, m=m: t[0] == m)
        if later:
            stage_of(0, later.pop(0))
    while later:
        stage_of(0, later.pop(0))
    while zw is None:
        zw = next(ar2)
    zw = expand(zw)
    qz = zw[:, :ntr].astype(BF16)
    wq = zw[:, ntr:].astype(BF16)
    y_add = SCALE * dot(qz[:rows_d], oum[...])
    for h in range(2):
        finish(0, h, y_add)
    produce(1, order[-1])
    add_core(1, order[-1])
    for h in range(2):
        pieces(1, h, 1, lambda t: t[0] == order[-1])
    x_add = SCALE * dot_nt(wq[:rows_d], idm[...])
    for i in range(2, nst):
        stage_of(1, i)
    odg[...] = SCALE * dot_tn(hid[...], vq)
    iug[0] = SCALE * dot_tn(q[:, :ntr], dgr[...])
    iug[1] = SCALE * dot_tn(q[:, ntr:], dur[...])
    for h in range(2):
        finish(1, h, x_add)
    oug[...] = SCALE * dot_tn(qz, held[0, 1])
    idg[...] = SCALE * dot_tn(held[0, 0], wq)
    out = wts[e][:, :1] * back[0, pl.ds(0, tok), :].astype(F32)
    for m in range(1, ne):
        for h in range(2):
            zret[0, h, m].wait_recv()
        out = out + wts[flip(e, m)][:, :1] * home[0, m].astype(F32)
    mixed[...] = out.astype(BF16)
    grad = back[1, pl.ds(0, tok), :].astype(F32)
    for m in range(1, ne):
        for h in range(2):
            zret[1, h, m].wait_recv()
        grad = grad + home[1, m].astype(F32)
    igrad[...] = grad.astype(BF16)
    for c in pending:
        c.wait_send()


def output_kernel(*refs):
    n = (len(refs) - 1) // 2
    copies = [pltpu.make_async_copy(refs[i], refs[n + i], refs[-1].at[i]) for i in range(n)]
    for c in copies:
        c.start()
    for c in copies:
        c.wait()


def per_device(
    tokens, out_grad, expert_ids, tenant_ids, router_logits,
    gate_projection_weight, up_projection_weight, down_projection_weight,
    input_down_maps, input_up_maps, output_down_map, output_up_map,
):
    ne, nd, nf = lax.axis_size("expert"), lax.axis_size("dp"), lax.axis_size("ffn")
    tok, quarter = tokens.shape
    hidden = gate_projection_weight.shape[2]
    ntr = output_down_map.shape[2]
    rows_d = ne * tok
    rows = nd * rows_d
    routes = orders(nd, nf)
    rs_bufs = []
    for r in routes:
        dims = [r[-1]] + r[:-1]
        for i in range(1, len(dims)):
            rs_bufs.append(pltpu.VMEM((2, len(received(dims, i, nd, nf)), rows_d, quarter // 2), BF16))
    n1, n2 = max(len(bits_of(nf)), 1), len(routes[0])
    n_sem = 2 * (ne - 1) + nd + ne * n2 + 2 * nd * nf * max(1, ne // 2 if ne <= 4 else 1)
    n_sem += n1 + n2 + 2 * nf + 4 * nd * nf + 4 * (ne - 1)
    vmem = pl.BlockSpec(memory_space=pltpu.VMEM)
    hbm = pl.BlockSpec(memory_space=pl.ANY)
    outs = (
        jax.ShapeDtypeStruct(tokens.shape, BF16),
        jax.ShapeDtypeStruct(tokens.shape, BF16),
        jax.ShapeDtypeStruct(input_down_maps.shape[1:], F32),
        jax.ShapeDtypeStruct(input_up_maps.shape[1:], F32),
        jax.ShapeDtypeStruct(output_down_map.shape[1:], F32),
        jax.ShapeDtypeStruct(output_up_map.shape[1:], F32),
    )
    scratch = [
        pltpu.VMEM(tokens.shape, BF16),
        pltpu.VMEM(tokens.shape, BF16),
        pltpu.VMEM(expert_ids.shape[::-1], jnp.int32),
        pltpu.VMEM((1, tok), jnp.int32),
        pltpu.VMEM(router_logits.shape[::-1], F32),
        pltpu.VMEM(input_down_maps.shape[1:], BF16),
        pltpu.VMEM(input_up_maps.shape[1:], BF16),
        pltpu.VMEM(output_down_map.shape[1:], BF16),
        pltpu.VMEM(output_up_map.shape[1:], BF16),
        pltpu.VMEM((ne, 2, tok, quarter), BF16),
        pltpu.VMEM((ne, tok, ntr), F32),
        pltpu.VMEM((ne, tok, LANES), F32),
        pltpu.VMEM((nf, 2, rows, quarter), BF16),
        pltpu.VMEM((nd, rows_d, ntr), F32),
        pltpu.VMEM((nf, quarter, hidden), BF16),
        pltpu.VMEM((nf, quarter, hidden), BF16),
        pltpu.VMEM((nf, hidden, quarter), BF16),
        pltpu.VMEM((rows, hidden), F32),
        pltpu.VMEM((rows, hidden), F32),
        pltpu.VMEM((rows, hidden), F32),
        pltpu.VMEM((rows, hidden), BF16),
        pltpu.VMEM((rows, hidden), BF16),
        pltpu.VMEM((rows, hidden), BF16),
        pltpu.VMEM((2, nf, rows, quarter), BF16),
        pltpu.VMEM((2, nf // 2, rows, quarter), BF16),
        pltpu.VMEM((2, rows_d, quarter), BF16),
        pltpu.VMEM((2, ne, tok, quarter), BF16),
        pltpu.VMEM((n1, rows, LANES), F32),
        pltpu.VMEM((n1, rows, LANES), F32),
        pltpu.VMEM((n2, rows, LANES), F32),
        pltpu.VMEM((n2, rows, LANES), F32),
        *rs_bufs,
        pltpu.SemaphoreType.DMA((9,)),
        pltpu.SemaphoreType.DMA((3 * nf,)),
        pltpu.SemaphoreType.DMA((n_sem,)),
        pltpu.SemaphoreType.DMA((n_sem,)),
    ]
    limit = 54 if rows <= 64 else 60
    parts = pl.pallas_call(
        functools.partial(layer_kernel, nd, ne, nf, tok),
        out_shape=tuple(pltpu.VMEM(o.shape, o.dtype) for o in outs),
        in_specs=[hbm] * 12,
        out_specs=[vmem] * 6,
        scratch_shapes=scratch,
        compiler_params=pltpu.CompilerParams(
            collective_id=0, has_side_effects=True, vmem_limit_bytes=limit * MIB
        ),
    )(
        tokens, out_grad, expert_ids.T, tenant_ids.reshape(1, tok), router_logits.T,
        gate_projection_weight, up_projection_weight, down_projection_weight,
        input_down_maps, input_up_maps, output_down_map, output_up_map,
    )
    mixed, igrad, idg, iug, odg, oug = pl.pallas_call(
        output_kernel,
        out_shape=outs,
        in_specs=[vmem] * 6,
        out_specs=[hbm] * 6,
        scratch_shapes=[pltpu.SemaphoreType.DMA((6,))],
        compiler_params=pltpu.CompilerParams(vmem_limit_bytes=8 * 1024 * 1024),
    )(*parts)
    return mixed, igrad, idg[None], iug[None], odg[None], oug[None]


MIB = 1 << 20


def solution(mesh):
    return jax.shard_map(
        per_device,
        mesh=mesh,
        in_specs=(
            P(("dp", "expert"), "ffn"),
            P(("dp", "expert"), "ffn"),
            P(("dp", "expert"), None),
            P(("dp", "expert")),
            P(("dp", "expert"), None),
            P("expert", None, ("dp", "ffn")),
            P("expert", None, ("dp", "ffn")),
            P("expert", ("dp", "ffn"), None),
            P("expert", "ffn", None),
            P("expert", None, None, ("dp", "ffn")),
            P("expert", ("dp", "ffn"), None),
            P("expert", None, "ffn"),
        ),
        out_specs=(
            P(("dp", "expert"), "ffn"),
            P(("dp", "expert"), "ffn"),
            P("expert", "ffn", None),
            P("expert", None, None, ("dp", "ffn")),
            P("expert", ("dp", "ffn"), None),
            P("expert", None, "ffn"),
        ),
        check_vma=False,
    )
```

time: 82 us -> 55.2 us (0.67)
  Pallas kernels: 74.5 us -> 54.3 us
  other arithmetic: 5.9 us -> 0 us
    pallas_call x2, Pallas kernels: 74.5 us -> 54.3 us  [the longest x1 52.3 us: per_device(): pl.pallas_call(functools.partial(layer_kernel, nd, ne, nf, tok), out_shap...]
    convert_element_type x3 -> x0, other arithmetic: 1.5 us -> none  [the longest x2 0.82 us: per_device(): dy = (weight[:, :, None] * out_grad.astype(F32)[None]).astype(BF16)]
    select_n x2 -> x0, other arithmetic: 0.82 us -> none  [the longest x1 0.82 us: per_device(): x = jnp.where(member[:, :, None], tokens[None], jnp.zeros((), BF16))]
where the time goes in v1:
time: 55.2 us; the launch traced here: 55 us
  Pallas kernels  54.3 us (98%)
  between operations  0.64 us (1%)
    pallas_call x1, Pallas kernels, per_device(): pl.pallas_call(functools.partial(layer_kernel, nd, ne, nf, tok), out_shap...  52.3 us
    pallas_call x1, Pallas kernels, per_device(): pl.pallas_call(output_kernel, out_shape=outs, in_specs=[vmem] * 6, out_sp...  1.99 us

profile of v1, /device:TPU:0, one launch (start us, length us, event | category | flops | bytes accessed | tf_op | source)
XLA Modules:
  0.0 55.0 jit_solution(9696954531877302043)
XLA Ops:
  0.6 52.3 %shard_map.163 = (bf16[8,1536]{1,0:T(8,128)(2,1)S(1)}, bf16[8,1536]{1,0:T(8,128)(2,1)S(1)}, f32[1536,256]{1,0:T(8,128)S(1)}, f32[2,128,1024]{2,1,0:T(8,128)S(1)}...) custom-call(bf16[8,1536]{1,0:T(8,128)(2,1)} %tokens.1, bf16[8,1536]{1,0:T(8,128)(2,1)} %out_grad.1, s32[2,8]{1,0:T(2,128)} %bitcast.7, ...), custom_call_target="tpu_custom_call" | custom-call | tf_op jit(solution)/shard_map/pallas_call | solution.py:530
  53.0 2.0 %shard_map.164 = (bf16[8,1536]{1,0:T(8,128)(2,1)}, bf16[8,1536]{1,0:T(8,128)(2,1)}, f32[1536,256]{1,0:T(8,128)}, f32[2,128,1024]{2,1,0:T(8,128)}, f32[1024,128]{1,0:T(8,128)}, /*index=5*/f32[128,1536]{1,0:T(8,128)}) custom-call(bf16[8,1536]{1,0:T(8,128)(2,1)S(1)} %get-tuple-element.18.refs_0_, bf16[8,1536]{1,0:T(8,128)(2,1)S(1)} %get-tuple-element.19.refs_1_, ...), custom_call_target="tpu_custom_call" | custom-call | tf_op jit(solution)/shard_map/pallas_call | solution.py:544
